TPU v7x, 256 devices: a 2x2x32 block of a 4x8x32 slice. The times are simulated.
256 devices in a mesh: parts: 4 (over y, x), dp: 64 (over z, core).
Axes of the slice: x: 2, y: 2, z: 32, core: 2. Of those that a mesh axis runs over, the one named last changes fastest.
The devices are a block of a 4x8x32 slice.
Arguments:
- activations: bfloat16 [65536, 14336], P(('parts', 'dp')), parts along dimension 0, may hold values from -6 to 6
- out_grads: bfloat16 [65536, 4096], P(('parts', 'dp')), parts along dimension 0, may hold values from -6 to 6
- lengths: int32 [256, 4], P(('parts', 'dp')), parts along dimension 0, may hold values from 1 to 128, 256 in all within a row
- proj_in: bfloat16 [14336, 64], replicated, may hold values from -0.046875 to 0.046875
- proj_out: bfloat16 [4096, 64], replicated, may hold values from -0.09375 to 0.09375
- queries: bfloat16 [8192, 4096], P(('parts', 'dp')), parts along dimension 0, may hold values from -0.01171875 to 0.01171875
Outputs:
- scores: bfloat16 [1024, 2048], P(('parts', 'dp')), parts along dimension 0
There are 4 independent parts, one for each index of `parts`. A program takes and returns all parts, laid end to end along the dimension named above; an argument that names none is the same for every part. Nothing has to cross between parts.
Inputs may be any that keep to these rules, and one draw needn't show every extreme that they name: Each row of lengths sums to 256, and one entry of each row equals 128.
All inputs are finite; a program needn't handle non-finite values.
Results may differ from a plain program's by a relative error of at most 0.0065.
Values may be sent and summed in bfloat16 or wider, within the bound.
A program may use at most 128 MiB of HBM per device.

v0:
```python
import jax
import jax.numpy as jnp
from jax import lax
from jax.sharding import PartitionSpec as P


def local(activations, out_grads, lengths, proj_in, proj_out, queries):
    tok_count = activations.shape[0]
    rank_size = proj_in.shape[1]
    proj_acts = jnp.dot(activations, proj_in, preferred_element_type=jnp.float32).astype(
        jnp.bfloat16
    )
    proj_grads = jnp.dot(out_grads, proj_out, preferred_element_type=jnp.float32).astype(
        jnp.bfloat16
    )
    counts = lengths[0]
    examples = counts.shape[0]
    position = jnp.arange(tok_count, dtype=jnp.int32)
    tok_ends = [counts[0]]
    for e in range(1, examples):
        tok_ends.append(tok_ends[-1] + counts[e])
    owner = sum(((position >= end).astype(jnp.int32) for end in tok_ends[:-1]))
    member = (owner[:, None] == jnp.arange(examples)[None, :]).astype(jnp.bfloat16)
    masked = (member[:, :, None] * proj_acts[:, None, :]).reshape(tok_count, examples * rank_size)
    summed = lax.dot_general(
        proj_grads, masked, (((0,), (0,)), ((), ())), preferred_element_type=jnp.float32
    )
    example_grads = (
        summed.reshape(rank_size, examples, rank_size)
        .transpose(1, 0, 2)
        .reshape(examples, rank_size * rank_size)
        .astype(jnp.bfloat16)
    )
    contract = (((1,), (1,)), ((), ()))
    scores = lax.dot_general(
        lax.all_gather(example_grads, "dp", axis=0, tiled=True),
        queries,
        contract,
        preferred_element_type=jnp.float32,
    ).astype(jnp.bfloat16)
    return lax.all_to_all(scores, "dp", split_axis=0, concat_axis=1, tiled=True)


def solution(mesh):
    in_specs = (
        P(("parts", "dp"), None),
        P(("parts", "dp"), None),
        P(("parts", "dp"), None),
        P(),
        P(),
        P(("parts", "dp"), None),
    )
    out_specs = P(("parts", "dp"), None)
    return jax.shard_map(local, mesh=mesh, in_specs=in_specs, out_specs=out_specs, check_vma=False)
```

profile of v0, /device:TPU:37, one launch (start us, length us, event | category | flops | bytes accessed | tf_op | source)
XLA Modules:
  0.0 216.6 jit_solution(11846224290307808529)
XLA Ops:
  6.5 0.0 copy-start
  6.6 0.0 all-gather.3.cloned.1.call-start
  6.6 1.4 fusion.9
  9.9 0.7 fusion.8
  10.6 0.0 copy-start.1
  10.6 6.0 %convolution_convert_fusion.1 = bf16[256,64]{0,1:T(8,128)(2,1)S(1)} fusion(bf16[256,14336]{1,0:T(8,128)(2,1)} %param.6, bf16[14336,64]{0,1:T(8,128)(2,1)} %param.9), kind=kOutput, calls=%fused_computation.2 | convolution fusion | flops 469778432 | bytes 9207808 | tf_op jit(solution)/shard_map/dot_general | solution.py:10
  16.6 0.0 copy-done
  16.6 0.0 copy-done.1
  16.6 1.0 fusion
  17.6 0.7 reshape.52
  18.3 0.1 all-gather.3.cloned.1.call-update
  18.4 0.0 copy-start.2
  18.4 145.2 %all-gather.3.cloned.1.call-done = bf16[64,4,4096]{2,1,0:T(4,128)(2,1)} async-done(((bf16[1,4,4096]{2,1,0:T(4,128)(2,1)}), bf16[64,4,4096]{2,1,0:T(4,128)(2,1)}) %all-gather.3.cloned.1.call-update) | async-done | bytes 2097168 | tf_op jit(solution)/shard_map/all_gather | solution.py:36
  163.6 4.0 %reshape.53 = bf16[256,4096]{1,0:T(8,128)(2,1)} reshape(bf16[64,4,4096]{2,1,0:T(4,128)(2,1)} %all-gather.3.cloned.1.call-done) | data formatting | bytes 4194304
  167.6 0.0 copy-done.2
  167.6 2.3 %convolution_convert_fusion.3 = bf16[256,32]{0,1:T(8,128)(2,1)S(1)} fusion(bf16[256,4096]{1,0:T(8,128)(2,1)} %reshape.53, bf16[32,4096]{1,0:T(8,128)(2,1)S(1)} %copy-done.2), kind=kOutput, calls=%fused_computation.5 | convolution fusion | flops 67117056 | bytes 2375680 | tf_op jit(solution)/shard_map/dot_general | solution.py:35
  169.9 0.1 copy.10
  170.0 39.0 %all_to_all.19 = bf16[64,4,32]{2,1,0:T(4,128)(2,1)S(1)} all-to-all(bf16[64,4,32]{2,1,0:T(4,128)(2,1)S(1)} %bitcast.24), channel_id=1, replica_groups=mesh['parts'=4,'dp'=64] {'dp'}, dimensions={0} | all-to-all | bytes 32768 | tf_op jit(solution)/shard_map/all_to_all | solution.py:41
  209.0 0.7 all_to_all.17
  (2 shorter events, 0.0 us)
Async XLA Ops:
  6.5 10.1 %copy-start = (bf16[256,4096]{1,0:T(8,128)(2,1)S(1)}, bf16[256,4096]{1,0:T(8,128)(2,1)}, u32[]{:S(2)}) copy-start(bf16[256,4096]{1,0:T(8,128)(2,1)} %param.7) | copy-start | bytes 6291460
  6.6 157.1 %all-gather.3.cloned.1.call-start = ((), (), s32[]{:S(2)}) async-start(), calls=%async_computation.1 | async-start | bytes 2129920 | tf_op jit(solution)/shard_map/all_gather | solution.py:36
  10.6 6.0 %copy-start.1 = (bf16[4096,64]{0,1:T(8,128)(2,1)S(1)}, bf16[4096,64]{0,1:T(8,128)(2,1)}, u32[]{:S(2)}) copy-start(bf16[4096,64]{0,1:T(8,128)(2,1)} %param.10) | copy-start | bytes 1572868
  18.4 149.2 %copy-start.2 = (bf16[32,4096]{1,0:T(8,128)(2,1)S(1)}, bf16[32,4096]{1,0:T(8,128)(2,1)}, u32[]{:S(2)}) copy-start(bf16[32,4096]{1,0:T(8,128)(2,1)} %param.11) | copy-start | bytes 786436
Sparse Core Ops, SparseCore 0:
  18.5 145.0 all-gather.2
where the time goes:
time: 217 us
  waiting for transfers between devices  145 us (67%)
  blocking collectives  39 us (18%)
  between operations  15.4 us (7%)
  matrix products  9.29 us (4%)
  local copies, waits for them, and re-layouts  7.01 us (3%)
    all_gather x1, waiting for transfers between devices, local(): lax.all_gather(example_grads, 'dp', axis=0, tiled=True)  145 us
    all_to_all x1, blocking collectives, local(): return lax.all_to_all(scores, 'dp', split_axis=0, concat_axis=1, tiled=True)  39 us
    dot_general x1, matrix products, local(): jnp.dot(activations, proj_in, preferred_element_type=jnp.float32)  5.99 us
    unnamed x8, local copies, waits for them, and re-layouts  4.71 us
  transfers between devices with their start and end apart: 1, of which 1 were waited for; matrix products, arithmetic and copies ran while one was open for 0% of the time, Pallas kernels for 0%

commit v1 on v0

--- a/solution.py
+++ b/solution.py
@@ -2,9 +2,15 @@
 import jax.numpy as jnp
 from jax import lax
 from jax.sharding import PartitionSpec as P
+from jax.lax import all_to_all, axis_size
 
 
 def local(activations, out_grads, lengths, proj_in, proj_out, queries):
+
+    def stacks_all_pack(piece_in):
+        r1 = jnp.concatenate(all_to_all(jnp.stack(axis_size("dp") * [piece_in]), "dp", 0, 0), 0)
+        return r1
+
     tok_count = activations.shape[0]
     rank_size = proj_in.shape[1]
     proj_acts = jnp.dot(activations, proj_in, preferred_element_type=jnp.float32).astype(
@@ -33,10 +39,7 @@
     )
     contract = (((1,), (1,)), ((), ()))
     scores = lax.dot_general(
-        lax.all_gather(example_grads, "dp", axis=0, tiled=True),
-        queries,
-        contract,
-        preferred_element_type=jnp.float32,
+        stacks_all_pack(example_grads), queries, contract, preferred_element_type=jnp.float32
     ).astype(jnp.bfloat16)
     return lax.all_to_all(scores, "dp", split_axis=0, concat_axis=1, tiled=True)
 

time: 217 us -> 283 us (1.30)
  blocking collectives: 39 us -> 263 us
  waiting for transfers between devices: 145 us -> 0 us
  between operations: 15.4 us -> 1.95 us
    all_to_all x0 -> x1, blocking collectives: none -> 232 us  [stacks_all_pack(): all_to_all(jnp.stack(axis_size('dp') * [piece_in]), 'dp', 0, 0)]
    all_gather x1 -> x0, waiting for transfers between devices: 145 us -> none  [local(): lax.all_gather(example_grads, 'dp', axis=0, tiled=True)]
    all_to_all x1, blocking collectives: 39 us -> 31.7 us  [local(): return lax.all_to_all(scores, 'dp', split_axis=0, concat_axis=1, tiled=True)]
    unnamed x8 -> x6, local copies, waits for them, and re-layouts: 4.71 us -> 0.01 us
    reshape x0 -> x1, local copies, waits for them, and re-layouts: none -> 3.99 us  [stacks_all_pack(): jnp.concatenate(all_to_all(jnp.stack(axis_size('dp') * [piece_in]), 'dp',...]
  transfers between devices with their start and end apart: 1 -> 0, of which waited for: 1 -> 0; matrix products, arithmetic and copies ran while one was open for 0% -> 0% of each run, Pallas kernels for 0% -> 0%
where the time goes in v1:
time: 283 us
  blocking collectives  263 us (93%)
  matrix products  9.29 us (3%)
  local copies, waits for them, and re-layouts  7.42 us (3%)
    all_to_all x1, blocking collectives, stacks_all_pack(): all_to_all(jnp.stack(axis_size('dp') * [piece_in]), 'dp', 0, 0)  232 us
    all_to_all x1, blocking collectives, local(): return lax.all_to_all(scores, 'dp', split_axis=0, concat_axis=1, tiled=True)  31.7 us
    dot_general x1, matrix products, local(): jnp.dot(activations, proj_in, preferred_element_type=jnp.float32)  5.99 us

profile of v1, /device:TPU:37, one launch (start us, length us, event | category | flops | bytes accessed | tf_op | source)
XLA Modules:
  0.0 282.5 jit_solution(8835142113678143529)
XLA Ops:
  0.0 0.0 copy-start
  0.0 1.4 fusion.9
  3.3 0.6 fusion.8
  3.9 0.0 copy-start.1
  4.0 6.0 %convolution_convert_fusion.1 = bf16[256,64]{0,1:T(8,128)(2,1)S(1)} fusion(bf16[256,14336]{1,0:T(8,128)(2,1)} %param.6, bf16[14336,64]{0,1:T(8,128)(2,1)} %param.9), kind=kOutput, calls=%fused_computation.2 | convolution fusion | flops 469778432 | bytes 9207808 | tf_op jit(solution)/shard_map/dot_general | solution.py:16
  9.9 0.0 copy-done
  10.0 0.0 copy-done.1
  10.0 1.0 fusion
  11.0 0.1 convert_element_type.56
  11.1 1.0 stack.2
  12.1 231.6 %all_to_all.24 = bf16[64,4,4096]{2,1,0:T(4,128)(2,1)} all-to-all(bf16[64,4,4096]{2,1,0:T(4,128)(2,1)S(1)} %stack.2), channel_id=1, replica_groups=mesh['parts'=4,'dp'=64] {'dp'}, dimensions={0} | all-to-all | bytes 4194304 | tf_op jit(solution)/shard_map/all_to_all | solution.py:11
  243.7 0.0 copy-start.2
  243.7 4.0 %reshape.58 = bf16[256,4096]{1,0:T(8,128)(2,1)} reshape(bf16[64,4,4096]{2,1,0:T(4,128)(2,1)} %all_to_all.24) | data formatting | bytes 4194304 | tf_op jit(solution)/shard_map/reshape | solution.py:11
  247.7 0.0 copy-done.2
  247.7 2.3 convolution_convert_fusion.3
  250.0 0.1 copy.8
  250.1 31.7 %all_to_all.25 = bf16[64,4,32]{2,1,0:T(4,128)(2,1)S(1)} all-to-all(bf16[64,4,32]{2,1,0:T(4,128)(2,1)S(1)} %bitcast.24), channel_id=1, replica_groups=mesh['parts'=4,'dp'=64] {'dp'}, dimensions={0} | all-to-all | bytes 32768 | tf_op jit(solution)/shard_map/all_to_all | solution.py:44
  281.8 0.7 all_to_all.21
  (2 shorter events, 0.0 us)
Async XLA Ops:
  0.0 9.9 %copy-start = (bf16[256,4096]{1,0:T(8,128)(2,1)S(1)}, bf16[256,4096]{1,0:T(8,128)(2,1)}, u32[]{:S(2)}) copy-start(bf16[256,4096]{1,0:T(8,128)(2,1)} %param.7) | copy-start | bytes 6291460
  3.9 6.0 %copy-start.1 = (bf16[4096,64]{0,1:T(8,128)(2,1)S(1)}, bf16[4096,64]{0,1:T(8,128)(2,1)}, u32[]{:S(2)}) copy-start(bf16[4096,64]{0,1:T(8,128)(2,1)} %param.10) | copy-start | bytes 1572868
  243.7 4.0 %copy-start.2 = (bf16[32,4096]{1,0:T(8,128)(2,1)S(1)}, bf16[32,4096]{1,0:T(8,128)(2,1)}, u32[]{:S(2)}) copy-start(bf16[32,4096]{1,0:T(8,128)(2,1)} %param.11) | copy-start | bytes 786436
